TPU v7x, 32 devices: a whole 2x2x4 slice. The times are simulated.
32 devices in a mesh: row: 4 (over y, core), col: 8 (over z, x).
Axes of the slice: x: 2, y: 2, z: 4, core: 2. Of those that a mesh axis runs over, the one named last changes fastest.
Arguments:
- phases: int32 [4, 8, 8, 24, 576], P('row', 'col'), may hold values from 0 to 2
- grain: float32 [4, 8, 8, 24, 576], P('row', 'col'), may hold values from 0.5 to 2
- phase_cond: float32 [3], replicated, may hold values from 0.3 to 3
- micro_counts: int32 [4, 8, 8], P('row', 'col'), may hold values from 6 to 12, as said below
- current: float32 [4, 8, 8], P('row', 'col'), may hold values from -5 to 5
- load: float32 [4, 8, 8], P('row', 'col'), may hold values from -16 to 16
Outputs:
- states: float32 [4, 8, 8, 3, 24, 576], P('row', 'col')
- tangent: float32 [4, 8, 8, 3, 3], P('row', 'col')
- increment: float32 [4, 8, 8], P('row', 'col')
- residual: float32 [4, 8, 8], P('row', 'col')
Inputs may be any that keep to these rules, and one draw needn't show every extreme that they name: `micro_counts`: every draw has an element with 12 inner iterations and one with 6.
All inputs are finite; a program needn't handle non-finite values.
Results may differ from a plain program's by a relative error of at most 0.0003.
Values sent between devices are 32-bit elements; how exact they have to be, the bound alone decides.
A program may use at most 64 MiB of HBM per device.

v0:
```python
import jax
import jax.numpy as jnp
from jax import lax
from jax.sharding import PartitionSpec as P

VOX = 24
YZ = 576
PHASES = 3
MACRO_ITERS = 8


def forward(field, axis_id):
    z_index = jnp.arange(YZ) % VOX
    if axis_id == 0:
        return jnp.roll(field, -1, axis=-2)
    if axis_id == 1:
        return jnp.roll(field, -VOX, axis=-1)
    return jnp.where(
        z_index == VOX - 1, jnp.roll(field, VOX - 1, axis=-1), jnp.roll(field, -1, axis=-1)
    )


def behind(field, axis_id):
    z_index = jnp.arange(YZ) % VOX
    if axis_id == 0:
        return jnp.roll(field, 1, axis=-2)
    if axis_id == 1:
        return jnp.roll(field, VOX, axis=-1)
    return jnp.where(z_index == 0, jnp.roll(field, 1 - VOX, axis=-1), jnp.roll(field, 1, axis=-1))


def solve_rve(conduct, count):
    faces = [(conduct + forward(conduct, axis_id)) * 0.5 for axis_id in range(3)]
    back_faces = [behind(faces[axis_id], axis_id) for axis_id in range(3)]
    rhs = jnp.stack([faces[axis_id] - back_faces[axis_id] for axis_id in range(3)])

    def operate(field):
        total = jnp.zeros_like(field)
        for axis_id in range(3):
            total = total + faces[axis_id] * (field - forward(field, axis_id))
            total = total + back_faces[axis_id] * (field - behind(field, axis_id))
        return total

    def sweep(index, carry):
        fluct, remain, direction, norm_now = carry
        image = operate(direction)
        step_size = norm_now / jnp.sum(direction * image, axis=(1, 2))
        fluct = fluct + step_size[:, None, None] * direction
        remain = remain - step_size[:, None, None] * image
        norm_next = jnp.sum(remain * remain, axis=(1, 2))
        direction = remain + (norm_next / norm_now)[:, None, None] * direction
        return (fluct, remain, direction, norm_next)

    start = (jnp.zeros_like(rhs), rhs, rhs, jnp.sum(rhs * rhs, axis=(1, 2)))
    fluct = lax.fori_loop(0, count, sweep, start)[0]
    identity = jnp.eye(3, dtype=conduct.dtype)
    rows_out = []
    for axis_id in range(3):
        flux = faces[axis_id][None] * (
            identity[axis_id][:, None, None] + forward(fluct, axis_id) - fluct
        )
        rows_out.append(jnp.mean(flux, axis=(1, 2)))
    return (fluct, jnp.stack(rows_out))


def solve_batch(conduct, counts):
    return lax.map(lambda pair: solve_rve(pair[0], pair[1]), (conduct, counts))


def neighbour(padded, axis_id, offset):
    lead = padded.ndim - 3
    index = [slice(None)] * lead + [slice(1, -1)] * 3
    length = padded.shape[lead + axis_id]
    index[lead + axis_id] = slice(1 + offset, length - 1 + offset)
    return padded[tuple(index)]


def coarse_apply(k_padded, v_padded):
    centre = neighbour(v_padded, 0, 0)
    total = jnp.zeros_like(centre)
    for axis_id in range(3):
        k_centre = neighbour(k_padded[axis_id], 0, 0)
        for offset in (1, -1):
            cond_face = 0.5 * (k_centre + neighbour(k_padded[axis_id], axis_id, offset))
            total = total + cond_face * (centre - neighbour(v_padded, axis_id, offset))
    return total


def coarse_cg(k_padded, residual, pad_field, norm_of, curv_of):
    increment = jnp.zeros_like(residual)
    direction = residual
    norm_now = norm_of(residual)
    for iteration in range(MACRO_ITERS):
        image = coarse_apply(k_padded, pad_field(direction))
        step_size = norm_now / curv_of(direction, image)
        increment = increment + step_size * direction
        residual = residual - step_size * image
        norm_next = norm_of(residual)
        direction = residual + norm_next / norm_now * direction
        norm_now = norm_next
    return (increment, residual)


def local_norm(field):
    return jnp.sum(field * field)


def local_curv(first, second):
    return jnp.sum(first * second)


def shards(phases, grain, phase_cond, micro_counts, current, load):
    depth = phases.shape[2]
    conduct = jnp.zeros(grain.shape, grain.dtype)
    for phase_id in range(PHASES):
        conduct = conduct + jnp.where(phases == phase_id, phase_cond[phase_id], 0.0)
    conduct = conduct * grain
    flat = conduct.reshape(depth, VOX, YZ)
    counts = micro_counts.reshape(depth)
    fluct, tangent = solve_batch(flat, counts)
    states = fluct.reshape(1, 1, depth, 3, VOX, YZ)
    tangent_out = tangent.reshape(1, 1, depth, 3, 3)
    diag = jnp.stack([tangent[:, axis_id, axis_id] for axis_id in range(3)]).reshape(3, 1, 1, depth)
    packed = jnp.concatenate(
        [diag, current.reshape(1, 1, 1, depth), load.reshape(1, 1, 1, depth)], axis=0
    ).reshape(5, 1, depth)
    whole = lax.all_gather(packed, ("row", "col"), axis=1, tiled=True)
    whole = whole.reshape(5, lax.axis_size("row"), lax.axis_size("col"), depth)
    padded = jnp.pad(whole, ((0, 0), (1, 1), (1, 1), (1, 1)))
    residual = whole[4] - coarse_apply(padded[:3], padded[3])
    increment, residual = coarse_cg(
        padded[:3], residual, lambda field: jnp.pad(field, 1), local_norm, local_curv
    )
    row_at = lax.axis_index("row")
    col_at = lax.axis_index("col")
    zero_at = jnp.zeros((), jnp.int32)
    increment = lax.dynamic_slice(increment, (row_at, col_at, zero_at), (1, 1, depth))
    residual = lax.dynamic_slice(residual, (row_at, col_at, zero_at), (1, 1, depth))
    return (states, tangent_out, increment, residual)


def solution(mesh):
    placed = (
        P("row", "col", None, None, None),
        P("row", "col", None, None, None),
        P(),
        P("row", "col", None),
        P("row", "col", None),
        P("row", "col", None),
    )
    return jax.shard_map(
        shards,
        mesh=mesh,
        in_specs=placed,
        out_specs=(
            P("row", "col", None, None, None, None),
            P("row", "col", None, None, None),
            P("row", "col", None),
            P("row", "col", None),
        ),
        check_vma=False,
    )
```

profile of v0, /device:TPU:0, one launch (start us, length us, event | category | flops | bytes accessed | tf_op | source)
XLA Modules:
  0.0 328.0 jit_solution(11989473639624334039)
XLA Ops:
  0.6 1.4 fusion.241
  2.0 3.3 multiply_bitcast_fusion.3
  5.3 194.7 %while.43 = (s32[]{:T(128)}, f32[8,3,24,576]{3,2,1,0:T(8,128)S(1)}, f32[8,3,3]{2,1,0:T(4,128)S(1)}, f32[8,24,576]{2,1,0:T(8,128)S(1)}, s32[8]{0:T(128)S(1)}, /*i...) while((s32[]{:T(128)}, f32[8,3,24,576]{3,2,1,0:T(8,128)S(1)}, f32[8,3,3]{2,1,0:T(4,128)S(1)}, ...), condition=%wide.region_9.10_spmd, body=%wide.region_0.9_spmd.sunk | while | flops 2898470 | bytes 12391870 | solution.py:67
  6.7 0.6 dynamic_slice.81
  7.3 26.4 %while.44 = (s32[]{:T(128)}, f32[3,24,576]{2,1,0:T(8,128)S(1)}, f32[3,24,576]{2,1,0:T(8,128)S(1)}, f32[3,24,576]{2,1,0:T(8,128)S(1)}, f32[3]{0:T(128)S(1)}, /*in...) while((s32[]{:T(128)}, f32[3,24,576]{2,1,0:T(8,128)S(1)}, ...), condition=%wide.region_5.5_spmd, body=%wide.region_2.4_spmd.sunk | while | flops 1539074 | bytes 5974553 | solution.py:55
  8.6 0.4 multiply_reduce_fusion.23
  10.8 0.4 multiply_reduce_fusion.23
  12.9 0.4 multiply_reduce_fusion.23
  15.1 0.4 multiply_reduce_fusion.23
  17.2 0.4 multiply_reduce_fusion.23
  19.4 0.4 multiply_reduce_fusion.23
  21.5 0.4 multiply_reduce_fusion.23
  23.7 0.4 multiply_reduce_fusion.23
  25.8 0.4 multiply_reduce_fusion.23
  28.0 0.4 multiply_reduce_fusion.23
  30.1 0.4 multiply_reduce_fusion.23
  32.3 0.4 multiply_reduce_fusion.23
  35.9 0.6 dynamic_slice.81
  36.5 13.5 %while.44 = (s32[]{:T(128)}, f32[3,24,576]{2,1,0:T(8,128)S(1)}, f32[3,24,576]{2,1,0:T(8,128)S(1)}, f32[3,24,576]{2,1,0:T(8,128)S(1)}, f32[3]{0:T(128)S(1)}, /*in...) while((s32[]{:T(128)}, f32[3,24,576]{2,1,0:T(8,128)S(1)}, ...), condition=%wide.region_5.5_spmd, body=%wide.region_2.4_spmd.sunk | while | flops 1539074 | bytes 5974553 | solution.py:55
  42.1 0.4 multiply_reduce_fusion.23
  52.2 0.6 dynamic_slice.81
  52.8 24.3 %while.44 = (s32[]{:T(128)}, f32[3,24,576]{2,1,0:T(8,128)S(1)}, f32[3,24,576]{2,1,0:T(8,128)S(1)}, f32[3,24,576]{2,1,0:T(8,128)S(1)}, f32[3]{0:T(128)S(1)}, /*in...) while((s32[]{:T(128)}, f32[3,24,576]{2,1,0:T(8,128)S(1)}, ...), condition=%wide.region_5.5_spmd, body=%wide.region_2.4_spmd.sunk | while | flops 1539074 | bytes 5974553 | solution.py:55
  54.1 0.4 multiply_reduce_fusion.23
  64.8 0.4 multiply_reduce_fusion.23
  75.6 0.4 multiply_reduce_fusion.23
  79.2 0.6 dynamic_slice.81
  79.8 22.1 %while.44 = (s32[]{:T(128)}, f32[3,24,576]{2,1,0:T(8,128)S(1)}, f32[3,24,576]{2,1,0:T(8,128)S(1)}, f32[3,24,576]{2,1,0:T(8,128)S(1)}, f32[3]{0:T(128)S(1)}, /*in...) while((s32[]{:T(128)}, f32[3,24,576]{2,1,0:T(8,128)S(1)}, ...), condition=%wide.region_5.5_spmd, body=%wide.region_2.4_spmd.sunk | while | flops 1539074 | bytes 5974553 | solution.py:55
  81.1 0.4 multiply_reduce_fusion.23
  91.9 0.4 multiply_reduce_fusion.23
  104.1 0.6 dynamic_slice.81
  104.7 24.3 %while.44 = (s32[]{:T(128)}, f32[3,24,576]{2,1,0:T(8,128)S(1)}, f32[3,24,576]{2,1,0:T(8,128)S(1)}, f32[3,24,576]{2,1,0:T(8,128)S(1)}, f32[3]{0:T(128)S(1)}, /*in...) while((s32[]{:T(128)}, f32[3,24,576]{2,1,0:T(8,128)S(1)}, ...), condition=%wide.region_5.5_spmd, body=%wide.region_2.4_spmd.sunk | while | flops 1539074 | bytes 5974553 | solution.py:55
  110.3 0.4 multiply_reduce_fusion.23
  121.0 0.4 multiply_reduce_fusion.23
  131.1 0.6 dynamic_slice.81
  131.7 20.0 %while.44 = (s32[]{:T(128)}, f32[3,24,576]{2,1,0:T(8,128)S(1)}, f32[3,24,576]{2,1,0:T(8,128)S(1)}, f32[3,24,576]{2,1,0:T(8,128)S(1)}, f32[3]{0:T(128)S(1)}, /*in...) while((s32[]{:T(128)}, f32[3,24,576]{2,1,0:T(8,128)S(1)}, ...), condition=%wide.region_5.5_spmd, body=%wide.region_2.4_spmd.sunk | while | flops 1539074 | bytes 5974553 | solution.py:55
  135.2 0.4 multiply_reduce_fusion.23
  143.8 0.4 multiply_reduce_fusion.23
  153.8 0.6 dynamic_slice.81
  154.4 22.1 %while.44 = (s32[]{:T(128)}, f32[3,24,576]{2,1,0:T(8,128)S(1)}, f32[3,24,576]{2,1,0:T(8,128)S(1)}, f32[3,24,576]{2,1,0:T(8,128)S(1)}, f32[3]{0:T(128)S(1)}, /*in...) while((s32[]{:T(128)}, f32[3,24,576]{2,1,0:T(8,128)S(1)}, ...), condition=%wide.region_5.5_spmd, body=%wide.region_2.4_spmd.sunk | while | flops 1539074 | bytes 5974553 | solution.py:55
  157.9 0.4 multiply_reduce_fusion.23
  168.6 0.4 multiply_reduce_fusion.23
  178.7 0.6 dynamic_slice.81
  179.3 20.0 %while.44 = (s32[]{:T(128)}, f32[3,24,576]{2,1,0:T(8,128)S(1)}, f32[3,24,576]{2,1,0:T(8,128)S(1)}, f32[3,24,576]{2,1,0:T(8,128)S(1)}, f32[3]{0:T(128)S(1)}, /*in...) while((s32[]{:T(128)}, f32[3,24,576]{2,1,0:T(8,128)S(1)}, ...), condition=%wide.region_5.5_spmd, body=%wide.region_2.4_spmd.sunk | while | flops 1539074 | bytes 5974553 | solution.py:55
  184.9 0.4 multiply_reduce_fusion.23
  193.5 0.4 multiply_reduce_fusion.23
  200.3 95.0 %all-gather = f32[5,32,1,8]{3,2,0,1:T(1,128)S(1)} all-gather(f32[5,1,1,8]{3,2,0,1:T(1,128)S(1)} %copy.37), channel_id=2, replica_groups=mesh['row'=4,'col'=8] {'row','col'}, dimensions={1}, use_global_device_ids=true | all-gather | bytes 5280 | tf_op jit(solution)/shard_map/all_gather | solution.py:127
  296.0 0.7 multiply_reduce_fusion.17
  298.0 0.6 multiply_reduce_fusion.16
  300.0 0.7 multiply_reduce_fusion.15
  302.0 0.6 multiply_reduce_fusion.14
  304.0 0.7 multiply_reduce_fusion.13
  306.0 0.6 multiply_reduce_fusion.12
  308.0 0.7 multiply_reduce_fusion.11
  310.0 0.6 multiply_reduce_fusion.10
  312.0 0.7 multiply_reduce_fusion.9
  314.0 0.6 multiply_reduce_fusion.8
  316.0 0.7 multiply_reduce_fusion.7
  318.0 0.6 multiply_reduce_fusion.6
  320.0 0.7 multiply_reduce_fusion.5
  322.0 0.6 multiply_reduce_fusion.4
  324.0 0.7 multiply_reduce_fusion.3
  326.1 0.6 copy.41
  326.7 0.6 copy.42
  327.3 0.7 copy.40
  (1524 shorter events, 116.2 us)
Async XLA Ops:
  0.6 4.7 %copy-start.3 = (s32[1,1,8]{2,1,0:T(1,128)S(1)}, s32[1,1,8]{2,1,0:T(1,128)}, u32[]{:S(2)}) copy-start(s32[1,1,8]{2,1,0:T(1,128)} %param.13) | copy-start | bytes 100
  5.3 195.0 %copy-start = (f32[1,1,8]{2,1,0:T(1,128)S(1)}, f32[1,1,8]{2,1,0:T(1,128)}, u32[]{:S(2)}) copy-start(f32[1,1,8]{2,1,0:T(1,128)} %param.15) | copy-start | bytes 100
  5.3 195.0 %copy-start.1 = (f32[1,1,8]{2,1,0:T(1,128)S(1)}, f32[1,1,8]{2,1,0:T(1,128)}, u32[]{:S(2)}) copy-start(f32[1,1,8]{2,1,0:T(1,128)} %param.14) | copy-start | bytes 100
  200.0 124.6 %copy-start.2 = (f32[8,3,24,576]{3,2,1,0:T(8,128)}, f32[8,3,24,576]{3,2,1,0:T(8,128)S(1)}, u32[]{:S(2)}) copy-start(f32[8,3,24,576]{3,2,1,0:T(8,128)S(1)} %get-tuple-element.269) | copy-start | bytes 3981316
where the time goes:
time: 330 us; the launch traced here: 328 us
  blocking collectives  95 us (29%)
  other arithmetic  84.9 us (26%)
  loops' own time  63.8 us (19%)
  local copies, waits for them, and re-layouts  63.4 us (19%)
  between operations  20.9 us (6%)
    all_gather x1, blocking collectives, shards(): whole = lax.all_gather(packed, ('row', 'col'), axis=1, tiled=True)  95 us
    another operation x8, loops' own time, solve_rve(): fluct = lax.fori_loop(0, count, sweep, start)[0]  61.7 us
    reduce_sum x78, other arithmetic, sweep(): step_size = norm_now / jnp.sum(direction * image, axis=(1, 2))  33 us
    reduce_sum x78, other arithmetic, sweep(): norm_next = jnp.sum(remain * remain, axis=(1, 2))  18.5 us
    slice x172, local copies, waits for them, and re-layouts, forward(): return jnp.roll(field, -VOX, axis=-1)  15.7 us
    slice x164, local copies, waits for them, and re-layouts, forward(): jnp.roll(field, VOX - 1, axis=-1)  15.1 us
    slice x172, local copies, waits for them, and re-layouts, forward(): jnp.roll(field, -1, axis=-1)  15 us
    add x78, other arithmetic, sweep(): direction = remain + (norm_next / norm_now)[:, None, None] * direction  10.1 us

commit v1 on v0

--- a/solution.py
+++ b/solution.py
@@ -124,7 +124,7 @@
     packed = jnp.concatenate(
         [diag, current.reshape(1, 1, 1, depth), load.reshape(1, 1, 1, depth)], axis=0
     ).reshape(5, 1, depth)
-    whole = lax.all_gather(packed, ("row", "col"), axis=1, tiled=True)
+    whole = jnp.concatenate(lax.all_gather(packed, ("row", "col")), axis=1)
     whole = whole.reshape(5, lax.axis_size("row"), lax.axis_size("col"), depth)
     padded = jnp.pad(whole, ((0, 0), (1, 1), (1, 1), (1, 1)))
     residual = whole[4] - coarse_apply(padded[:3], padded[3])

time: 330 us -> 330 us (level)
  no operation moved by 1% of the time
where the time goes in v1:
time: 330 us; the launch traced here: 329 us
  blocking collectives  95 us (29%)
  other arithmetic  84.9 us (26%)
  local copies, waits for them, and re-layouts  63.8 us (19%)
  loops' own time  63.8 us (19%)
  between operations  20.9 us (6%)
    all_gather x1, blocking collectives, shards(): whole = jnp.concatenate(lax.all_gather(packed, ('row', 'col')), axis=1)  95 us
    another operation x8, loops' own time, solve_rve(): fluct = lax.fori_loop(0, count, sweep, start)[0]  61.7 us
    reduce_sum x78, other arithmetic, sweep(): step_size = norm_now / jnp.sum(direction * image, axis=(1, 2))  33 us
    reduce_sum x78, other arithmetic, sweep(): norm_next = jnp.sum(remain * remain, axis=(1, 2))  18.5 us
    slice x172, local copies, waits for them, and re-layouts, forward(): return jnp.roll(field, -VOX, axis=-1)  15.7 us
    slice x164, local copies, waits for them, and re-layouts, forward(): jnp.roll(field, VOX - 1, axis=-1)  15.1 us
    slice x172, local copies, waits for them, and re-layouts, forward(): jnp.roll(field, -1, axis=-1)  15 us
    add x78, other arithmetic, sweep(): direction = remain + (norm_next / norm_now)[:, None, None] * direction  10.1 us

profile of v1, /device:TPU:0, one launch (start us, length us, event | category | flops | bytes accessed | tf_op | source)
XLA Modules:
  0.0 328.5 jit_solution(16228874044277907335)
XLA Ops:
  0.6 1.4 fusion.241
  2.0 3.3 multiply_bitcast_fusion.3
  5.3 194.7 %while.43 = (s32[]{:T(128)}, f32[8,3,24,576]{3,2,1,0:T(8,128)S(1)}, f32[8,3,3]{2,1,0:T(4,128)S(1)}, f32[8,24,576]{2,1,0:T(8,128)S(1)}, s32[8]{0:T(128)S(1)}, /*i...) while((s32[]{:T(128)}, f32[8,3,24,576]{3,2,1,0:T(8,128)S(1)}, f32[8,3,3]{2,1,0:T(4,128)S(1)}, ...), condition=%wide.region_9.10_spmd, body=%wide.region_0.9_spmd.sunk | while | flops 2898470 | bytes 12391870 | solution.py:67
  6.7 0.6 dynamic_slice.81
  7.3 26.4 %while.44 = (s32[]{:T(128)}, f32[3,24,576]{2,1,0:T(8,128)S(1)}, f32[3,24,576]{2,1,0:T(8,128)S(1)}, f32[3,24,576]{2,1,0:T(8,128)S(1)}, f32[3]{0:T(128)S(1)}, /*in...) while((s32[]{:T(128)}, f32[3,24,576]{2,1,0:T(8,128)S(1)}, ...), condition=%wide.region_5.5_spmd, body=%wide.region_2.4_spmd.sunk | while | flops 1539074 | bytes 5974553 | solution.py:55
  8.6 0.4 multiply_reduce_fusion.23
  10.8 0.4 multiply_reduce_fusion.23
  12.9 0.4 multiply_reduce_fusion.23
  15.1 0.4 multiply_reduce_fusion.23
  17.2 0.4 multiply_reduce_fusion.23
  19.4 0.4 multiply_reduce_fusion.23
  21.5 0.4 multiply_reduce_fusion.23
  23.7 0.4 multiply_reduce_fusion.23
  25.8 0.4 multiply_reduce_fusion.23
  28.0 0.4 multiply_reduce_fusion.23
  30.1 0.4 multiply_reduce_fusion.23
  32.3 0.4 multiply_reduce_fusion.23
  35.9 0.6 dynamic_slice.81
  36.5 13.5 %while.44 = (s32[]{:T(128)}, f32[3,24,576]{2,1,0:T(8,128)S(1)}, f32[3,24,576]{2,1,0:T(8,128)S(1)}, f32[3,24,576]{2,1,0:T(8,128)S(1)}, f32[3]{0:T(128)S(1)}, /*in...) while((s32[]{:T(128)}, f32[3,24,576]{2,1,0:T(8,128)S(1)}, ...), condition=%wide.region_5.5_spmd, body=%wide.region_2.4_spmd.sunk | while | flops 1539074 | bytes 5974553 | solution.py:55
  42.1 0.4 multiply_reduce_fusion.23
  52.2 0.6 dynamic_slice.81
  52.8 24.3 %while.44 = (s32[]{:T(128)}, f32[3,24,576]{2,1,0:T(8,128)S(1)}, f32[3,24,576]{2,1,0:T(8,128)S(1)}, f32[3,24,576]{2,1,0:T(8,128)S(1)}, f32[3]{0:T(128)S(1)}, /*in...) while((s32[]{:T(128)}, f32[3,24,576]{2,1,0:T(8,128)S(1)}, ...), condition=%wide.region_5.5_spmd, body=%wide.region_2.4_spmd.sunk | while | flops 1539074 | bytes 5974553 | solution.py:55
  54.1 0.4 multiply_reduce_fusion.23
  64.8 0.4 multiply_reduce_fusion.23
  75.6 0.4 multiply_reduce_fusion.23
  79.2 0.6 dynamic_slice.81
  79.8 22.1 %while.44 = (s32[]{:T(128)}, f32[3,24,576]{2,1,0:T(8,128)S(1)}, f32[3,24,576]{2,1,0:T(8,128)S(1)}, f32[3,24,576]{2,1,0:T(8,128)S(1)}, f32[3]{0:T(128)S(1)}, /*in...) while((s32[]{:T(128)}, f32[3,24,576]{2,1,0:T(8,128)S(1)}, ...), condition=%wide.region_5.5_spmd, body=%wide.region_2.4_spmd.sunk | while | flops 1539074 | bytes 5974553 | solution.py:55
  81.1 0.4 multiply_reduce_fusion.23
  91.9 0.4 multiply_reduce_fusion.23
  104.1 0.6 dynamic_slice.81
  104.7 24.3 %while.44 = (s32[]{:T(128)}, f32[3,24,576]{2,1,0:T(8,128)S(1)}, f32[3,24,576]{2,1,0:T(8,128)S(1)}, f32[3,24,576]{2,1,0:T(8,128)S(1)}, f32[3]{0:T(128)S(1)}, /*in...) while((s32[]{:T(128)}, f32[3,24,576]{2,1,0:T(8,128)S(1)}, ...), condition=%wide.region_5.5_spmd, body=%wide.region_2.4_spmd.sunk | while | flops 1539074 | bytes 5974553 | solution.py:55
  110.3 0.4 multiply_reduce_fusion.23
  121.0 0.4 multiply_reduce_fusion.23
  131.1 0.6 dynamic_slice.81
  131.7 20.0 %while.44 = (s32[]{:T(128)}, f32[3,24,576]{2,1,0:T(8,128)S(1)}, f32[3,24,576]{2,1,0:T(8,128)S(1)}, f32[3,24,576]{2,1,0:T(8,128)S(1)}, f32[3]{0:T(128)S(1)}, /*in...) while((s32[]{:T(128)}, f32[3,24,576]{2,1,0:T(8,128)S(1)}, ...), condition=%wide.region_5.5_spmd, body=%wide.region_2.4_spmd.sunk | while | flops 1539074 | bytes 5974553 | solution.py:55
  135.2 0.4 multiply_reduce_fusion.23
  143.8 0.4 multiply_reduce_fusion.23
  153.8 0.6 dynamic_slice.81
  154.4 22.1 %while.44 = (s32[]{:T(128)}, f32[3,24,576]{2,1,0:T(8,128)S(1)}, f32[3,24,576]{2,1,0:T(8,128)S(1)}, f32[3,24,576]{2,1,0:T(8,128)S(1)}, f32[3]{0:T(128)S(1)}, /*in...) while((s32[]{:T(128)}, f32[3,24,576]{2,1,0:T(8,128)S(1)}, ...), condition=%wide.region_5.5_spmd, body=%wide.region_2.4_spmd.sunk | while | flops 1539074 | bytes 5974553 | solution.py:55
  157.9 0.4 multiply_reduce_fusion.23
  168.6 0.4 multiply_reduce_fusion.23
  178.7 0.6 dynamic_slice.81
  179.3 20.0 %while.44 = (s32[]{:T(128)}, f32[3,24,576]{2,1,0:T(8,128)S(1)}, f32[3,24,576]{2,1,0:T(8,128)S(1)}, f32[3,24,576]{2,1,0:T(8,128)S(1)}, f32[3]{0:T(128)S(1)}, /*in...) while((s32[]{:T(128)}, f32[3,24,576]{2,1,0:T(8,128)S(1)}, ...), condition=%wide.region_5.5_spmd, body=%wide.region_2.4_spmd.sunk | while | flops 1539074 | bytes 5974553 | solution.py:55
  184.9 0.4 multiply_reduce_fusion.23
  193.5 0.4 multiply_reduce_fusion.23
  200.3 95.0 %all-gather = f32[160,1,1,8]{3,2,1,0:T(1,128)S(1)} all-gather(f32[5,1,1,8]{3,2,1,0:T(1,128)S(1)} %copy.41), channel_id=2, replica_groups=mesh['row'=4,'col'=8] {'row','col'}, dimensions={0}, use_global_device_ids=true | all-gather | bytes 5280 | tf_op jit(solution)/shard_map/all_gather | solution.py:127
  296.5 0.7 multiply_reduce_fusion.17
  298.5 0.6 multiply_reduce_fusion.16
  300.5 0.7 multiply_reduce_fusion.15
  302.5 0.6 multiply_reduce_fusion.14
  304.5 0.7 multiply_reduce_fusion.13
  306.5 0.6 multiply_reduce_fusion.12
  308.5 0.7 multiply_reduce_fusion.11
  310.5 0.6 multiply_reduce_fusion.10
  312.5 0.7 multiply_reduce_fusion.9
  314.5 0.6 multiply_reduce_fusion.8
  316.5 0.7 multiply_reduce_fusion.7
  318.5 0.6 multiply_reduce_fusion.6
  320.5 0.7 multiply_reduce_fusion.5
  322.5 0.6 multiply_reduce_fusion.4
  324.5 0.7 multiply_reduce_fusion.3
  326.7 0.6 copy.45
  327.2 0.6 copy.46
  327.8 0.7 copy.44
  (1525 shorter events, 116.7 us)
Async XLA Ops:
  0.6 4.7 %copy-start.3 = (s32[1,1,8]{2,1,0:T(1,128)S(1)}, s32[1,1,8]{2,1,0:T(1,128)}, u32[]{:S(2)}) copy-start(s32[1,1,8]{2,1,0:T(1,128)} %param.13) | copy-start | bytes 100
  5.3 195.0 %copy-start = (f32[1,1,8]{2,1,0:T(1,128)S(1)}, f32[1,1,8]{2,1,0:T(1,128)}, u32[]{:S(2)}) copy-start(f32[1,1,8]{2,1,0:T(1,128)} %param.15) | copy-start | bytes 100
  5.3 195.0 %copy-start.1 = (f32[1,1,8]{2,1,0:T(1,128)S(1)}, f32[1,1,8]{2,1,0:T(1,128)}, u32[]{:S(2)}) copy-start(f32[1,1,8]{2,1,0:T(1,128)} %param.14) | copy-start | bytes 100
  200.0 121.1 %copy-start.2 = (f32[8,3,24,576]{3,2,1,0:T(8,128)}, f32[8,3,24,576]{3,2,1,0:T(8,128)S(1)}, u32[]{:S(2)}) copy-start(f32[8,3,24,576]{3,2,1,0:T(8,128)S(1)} %get-tuple-element.269) | copy-start | bytes 3981316
